TPU v7x, 32 devices: a whole 2x2x4 slice. The times are simulated.
32 devices in a mesh: ia: 4 (over y, x), ja: 4 (over z), col: 2 (over core).
Axes of the slice: x: 2, y: 2, z: 4, core: 2. Of those that a mesh axis runs over, the one named last changes fastest.
Arguments:
- pair_rep: bfloat16 [512, 512, 128], P('ia', 'ja'), may hold values from -6 to 6
- norm_gain: float32 [128], replicated, may hold values from 0.1 to 1.9
- weights: bfloat16 [4, 128, 128], P(None, None, 'col'), may hold values from -0.5 to 0.5
- residue_mask: int32 [512], replicated, may hold values 0 or 1
- product_grad: bfloat16 [512, 128, 512], P('ia', 'col', 'ja'), may hold values from -1 to 1
Outputs:
- pair_grad: bfloat16 [512, 512, 128], P('ia', 'ja')
- weight_grads: float32 [4, 128, 128], P(None, None, 'col')
All inputs are finite; a program needn't handle non-finite values.
Results may differ from a plain program's by a relative error of at most 0.0067.
Values may be sent and summed in bfloat16 or wider, within the bound.
A program may use at most 128 MiB of HBM per device.

v0:
```python
import jax
import jax.numpy as jnp
from jax import lax
from jax.sharding import PartitionSpec as P

CLIP_LIMIT = 64.0


def gate_terms(incoming, linear, gate_pre, pair_valid):
    sigmoid_gate = jax.nn.sigmoid(gate_pre)
    through = incoming * pair_valid
    return (through * sigmoid_gate, through * linear * sigmoid_gate * (1.0 - sigmoid_gate))


def on_device(pair_rep, norm_gain, weights, residue_mask, product_grad):
    row_count = pair_rep.shape[0]
    col_count = pair_rep.shape[1]
    row_first = lax.axis_index("ia") * row_count
    col_first = lax.axis_index("ja") * col_count
    validity = residue_mask.astype(jnp.float32)
    row_valid = lax.dynamic_slice_in_dim(validity, row_first, row_count)
    col_valid = lax.dynamic_slice_in_dim(validity, col_first, col_count)
    pair_valid = row_valid[:, None, None] * col_valid[None, None, :]
    floats = pair_rep.astype(jnp.float32)
    centred = floats - jnp.mean(floats, axis=-1, keepdims=True)
    inv_std = lax.rsqrt(jnp.mean(centred * centred, axis=-1, keepdims=True) + 1e-05)
    unit_rows = centred * inv_std
    normed = (unit_rows * norm_gain).astype(jnp.bfloat16)
    projected = jnp.einsum("ikd,wdc->wick", normed, weights, preferred_element_type=jnp.float32)
    left_side = (pair_valid * jax.nn.sigmoid(projected[1]) * projected[0]).astype(jnp.bfloat16)
    right_side = (pair_valid * jax.nn.sigmoid(projected[3]) * projected[2]).astype(jnp.bfloat16)
    row_panel = lax.all_gather(product_grad, "ja", axis=2, tiled=True)
    panel_part = row_panel
    grad_left = jnp.einsum(
        "icj,jck->ick",
        panel_part,
        lax.all_gather(right_side, "ia", axis=0, tiled=True),
        preferred_element_type=jnp.float32,
    )
    panel_part = row_panel
    grad_right = lax.psum_scatter(
        jnp.einsum("icj,ick->jck", panel_part, left_side, preferred_element_type=jnp.float32),
        "ia",
        scatter_dimension=0,
        tiled=True,
    )
    lin_a, gate_a = gate_terms(grad_left, projected[0], projected[1], pair_valid)
    lin_b, gate_b = gate_terms(grad_right, projected[2], projected[3], pair_valid)
    proj_grads = jnp.stack([lin_a, gate_a, lin_b, gate_b]).astype(jnp.bfloat16)
    grad_part = jnp.einsum("ikd,wick->wdc", normed, proj_grads, preferred_element_type=jnp.float32)
    input_part = jnp.einsum(
        "wick,wdc->ikd", proj_grads, weights, preferred_element_type=jnp.float32
    )
    normed_grad = lax.psum(input_part, "col")
    scaled = normed_grad * norm_gain
    pair_grad = inv_std * (
        scaled
        - jnp.mean(scaled, axis=-1, keepdims=True)
        - unit_rows * jnp.mean(scaled * unit_rows, axis=-1, keepdims=True)
    )
    summed = lax.psum(grad_part, ("ia", "ja"))
    squares = lax.psum(jnp.sum(summed * summed), "col")
    factor = jnp.minimum(1.0, CLIP_LIMIT * lax.rsqrt(squares + 1e-06))
    weight_grads = summed * factor
    return (pair_grad.astype(jnp.bfloat16), weight_grads)


def solution(mesh):
    placed = (P("ia", "ja", None), P(), P(None, None, "col"), P(), P("ia", "col", "ja"))
    return jax.shard_map(
        on_device,
        mesh=mesh,
        in_specs=placed,
        out_specs=(P("ia", "ja", None), P(None, None, "col")),
        check_vma=False,
    )
```

profile of v0, /device:TPU:0, one launch (start us, length us, event | category | flops | bytes accessed | tf_op | source)
XLA Modules:
  0.0 660.3 jit_solution(14896707460684824877)
XLA Ops:
  7.2 4.3 copy.18
  11.8 3.5 convert_reduce_fusion
  15.3 4.8 fusion.10
  20.2 4.7 convolution_bitcast_fusion
  24.9 5.9 copy-done.1
  30.8 2.6 multiply_convert_fusion.5
  33.9 129.6 %all-gather.5.cloned.1.call-done = bf16[128,64,512]{2,0,1:T(8,128)(2,1)} async-done(((bf16[128,64,128]{2,0,1:T(8,128)(2,1)}), bf16[128,64,512]{2,0,1:T(8,128)(2,1)}) %all-gather.5.cloned.1.call-update) | async-done | bytes 8388624 | tf_op jit(solution)/shard_map/all_gather | solution.py:32
  163.5 87.5 %all-gather.3.cloned.1.call-done = bf16[512,64,128]{2,1,0:T(8,128)(2,1)} async-done(((bf16[128,64,128]{2,1,0:T(8,128)(2,1)}), bf16[512,64,128]{2,1,0:T(8,128)(2,1)}) %all-gather.3.cloned.1.call-update) | async-done | bytes 8388624 | tf_op jit(solution)/shard_map/all_gather | solution.py:37
  251.0 25.2 %fusion.11 = f32[64,128,128]{2,1,0:T(8,128)} fusion(bf16[128,64,512]{2,0,1:T(8,128)(2,1)} %all-gather.5.cloned.1.call-done, bf16[512,64,128]{2,1,0:T(8,128)(2,1)} %all-gather.3.cloned.1.call-done), kind=kOutput, calls=%fused_computation.15 | convolution fusion | flops 1073741824 | bytes 20971520 | tf_op jit(solution)/shard_map/icj,jck->ick/dot_general | solution.py:34
  276.2 5.4 copy.20
  281.6 6.8 %fusion.28 = (bf16[1,128,64,128]{3,2,1,0:T(8,128)(2,1)S(1)}, bf16[1,128,64,128]{3,2,1,0:T(8,128)(2,1)}, bf16[128,64,128]{2,1,0:T(8,128)(2,1)S(1)}) fusion(f32[64,128,128]{1,0,2:T(8,128)} %copy.20, f32[128,128]{1,0:T(8,128)S(1)} %broadcast_multiply_fusion.1, f32[4,128,64,128]{3,2,0,1:T(8,128)} %copy-done.1), kind=kLoop, calls=%fused_computation.43 | loop fusion | flops 14680064 | bytes 18939904 | tf_op jit(solution)/shard_map/stack | solution.py:49
  288.5 14.1 %fusion.32 = f32[64,128,512]{2,1,0:T(8,128)} fusion(bf16[128,64,512]{2,0,1:T(8,128)(2,1)} %all-gather.5.cloned.1.call-done, bf16[128,64,128]{2,1,0:T(8,128)(2,1)S(1)} %get-tuple-element.8), kind=kOutput, calls=%fused_computation.47 | convolution fusion | flops 1073741824 | bytes 27262976 | tf_op jit(solution)/shard_map/icj,ick->jck/dot_general | solution.py:42
  302.6 16.6 %copy.23 = f32[64,128,512]{1,0,2:T(8,128)} copy(f32[64,128,512]{2,1,0:T(8,128)} %fusion.32) | data formatting | bytes 33554432 | tf_op jit(solution)/shard_map/icj,ick->jck/dot_general | solution.py:42
  319.2 153.8 %reduce-scatter.2.cloned.1.call-done = f32[128,64,128]{2,1,0:T(8,128)} async-done(((f32[512,64,128]{2,1,0:T(8,128)}), f32[128,64,128]{2,1,0:T(8,128)}) %reduce-scatter.2.cloned.1.call-update) | async-done | bytes 4194320 | tf_op jit(solution)/shard_map/reduce_scatter | solution.py:41
  473.1 6.0 fusion.30
  481.1 5.4 fusion.34
  486.6 6.5 convolution_bitcast_fusion.1
  493.1 99.0 %all-reduce.5.cloned.1.call-done = f32[4,128,64]{1,2,0:T(8,128)} async-done(((f32[4,128,64]{1,2,0:T(8,128)}), f32[4,128,64]{1,2,0:T(8,128)}) %all-reduce.5.cloned.1.call-update) | async-done | bytes 131088 | tf_op jit(solution)/shard_map/psum | solution.py:61
  592.1 1.5 multiply_reduce_fusion.1
  593.7 3.1 psum.23
  597.4 1.6 broadcast_multiply_fusion
  599.0 32.2 %all-reduce.3.cloned.1.call-done = f32[128,128,128]{2,1,0:T(8,128)} async-done(((f32[128,128,128]{2,1,0:T(8,128)}), f32[128,128,128]{2,1,0:T(8,128)}) %all-reduce.3.cloned.1.call-update) | async-done | bytes 8388624 | tf_op jit(solution)/shard_map/psum | solution.py:54
  631.2 11.6 %multiply_reduce_fusion = (f32[128,128]{1,0:T(8,128)S(1)}, f32[128,128]{1,0:T(8,128)S(1)}) fusion(f32[128,128,128]{2,1,0:T(8,128)} %all-reduce.3.cloned.1.call-done, f32[128]{0:T(128)S(1)} %copy-done.9, f32[128,128]{1,0:T(8,128)S(1)} %add_rsqrt_fusion, f32[128,128]{1,0:T(8,128)S(1)} %broadcast_multiply_fusion.4, bf16[128,128,128]{2,1,0:T(8,128)(2,1)} %param.5), kind=kLoop, calls=%fused_computation.17 | loop fusion | flops 14647296 | bytes 12845568 | tf_op jit(solution)/shard_map/reduce_sum | solution.py:58
  642.8 10.7 %fusion.9 = bf16[128,128,128]{2,1,0:T(8,128)(2,1)} fusion(bf16[128,128,128]{2,1,0:T(8,128)(2,1)S(1)} %copy-done.4, f32[128,128,128]{2,1,0:T(8,128)S(1)} %copy-done.5, f32[128,128]{1,0:T(8,128)S(1)} %get-tuple-element.11, f32[128,128]{1,0:T(8,128)S(1)} %get-tuple-element.12, f32[128]{0:T(128)S(1)} %copy-done.9, f32[128,128]{1,0:T(8,128)S(1)} %add_rsqrt_fusion, ...), kind=kLoop, calls=%fused_computation.12 | loop fusion | flops 18874368 | bytes 17039872 | tf_op jit(solution)/shard_map/convert_element_type | solution.py:65
  (37 shorter events, 3.0 us)
Async XLA Ops:
  7.2 13.0 %copy-start = (bf16[4,128,64]{1,2,0:T(8,128)(2,1)S(1)}, bf16[4,128,64]{1,2,0:T(8,128)(2,1)}, u32[]{:S(2)}) copy-start(bf16[4,128,64]{1,2,0:T(8,128)(2,1)} %param.7) | copy-start | bytes 196612
  7.2 4.4 copy-start.10
  7.2 156.3 %all-gather.5.cloned.1.call-start = ((), (), s32[]{:S(2)}) async-start(), calls=%async_computation.2 | async-start | bytes 10485760 | tf_op jit(solution)/shard_map/all_gather | solution.py:32
  11.5 239.5 %all-gather.3.cloned.1.call-start = ((), (), s32[]{:S(2)}) async-start(), calls=%async_computation.1 | async-start | bytes 10485760 | tf_op jit(solution)/shard_map/all_gather | solution.py:37
  11.6 3.7 copy-start.2
  11.8 8.4 %copy-start.9 = (f32[128]{0:T(128)S(1)}, f32[128]{0:T(128)}, u32[]{:S(2)}) copy-start(f32[128]{0:T(128)} %param.6) | copy-start | bytes 1540
  24.9 5.9 copy-start.1
  33.4 439.6 %reduce-scatter.2.cloned.1.call-start = ((), (), s32[]{:S(2)}) async-start(), calls=%async_computation.3 | async-start | bytes 20971520 | tf_op jit(solution)/shard_map/reduce_scatter | solution.py:41
  319.2 272.9 %all-reduce.5.cloned.1.call-start = ((), (), s32[]{:S(2)}) async-start(), calls=%async_computation.5 | async-start | bytes 262144 | tf_op jit(solution)/shard_map/psum | solution.py:61
  473.1 8.0 %copy-start.3 = (bf16[128,128,128]{2,1,0:T(8,128)(2,1)S(1)}, bf16[128,128,128]{2,1,0:T(8,128)(2,1)}, u32[]{:S(2)}) copy-start(bf16[128,128,128]{2,1,0:T(8,128)(2,1)} %param.5) | copy-start | bytes 12582916
  473.1 8.0 %copy-start.6 = (bf16[1,128,64,128]{3,2,1,0:T(8,128)(2,1)S(1)}, bf16[1,128,64,128]{3,2,1,0:T(8,128)(2,1)}, u32[]{:S(2)}) copy-start(bf16[1,128,64,128]{3,2,1,0:T(8,128)(2,1)} %get-tuple-element.5) | copy-start | bytes 6291460
  479.1 1.3 copy-start.7
  479.1 2.0 copy-start.8
  486.6 144.6 %all-reduce.3.cloned.1.call-start = ((), (), s32[]{:S(2)}) async-start(), calls=%async_computation.4 | async-start | bytes 16777216 | tf_op jit(solution)/shard_map/psum | solution.py:54
  631.2 11.6 %copy-start.4 = (bf16[128,128,128]{2,1,0:T(8,128)(2,1)S(1)}, bf16[128,128,128]{2,1,0:T(8,128)(2,1)}, u32[]{:S(2)}) copy-start(bf16[128,128,128]{2,1,0:T(8,128)(2,1)} %param.5) | copy-start | bytes 12582916
  631.2 11.6 %copy-start.5 = (f32[128,128,128]{2,1,0:T(8,128)S(1)}, f32[128,128,128]{2,1,0:T(8,128)}, u32[]{:S(2)}) copy-start(f32[128,128,128]{2,1,0:T(8,128)} %all-reduce.3.cloned.1.call-done) | copy-start | bytes 25165828
Sparse Core Ops, SparseCore 0:
  11.6 151.8 all-gather.4
  165.4 85.6 all-gather.2
  319.3 153.7 reduce-scatter.1
  486.7 105.3 all-reduce.4
  594.4 36.6 all-reduce.2
where the time goes:
time: 668 us; the launch traced here: 660 us
  waiting for transfers between devices  502 us (75%)
  matrix products  55.9 us (8%)
  other arithmetic  49.3 us (7%)
  local copies, waits for them, and re-layouts  34.2 us (5%)
  between operations  14.9 us (2%)
    reduce_scatter x1, waiting for transfers between devices, on_device(): lax.psum_scatter(jnp.einsum('icj,ick->jck', panel_part, left_side, prefer...  154 us
    all_gather x1, waiting for transfers between devices, on_device(): row_panel = lax.all_gather(product_grad, 'ja', axis=2, tiled=True)  130 us
    psum x1, waiting for transfers between devices, on_device(): summed = lax.psum(grad_part, ('ia', 'ja'))  99 us
    all_gather x1, waiting for transfers between devices, on_device(): lax.all_gather(right_side, 'ia', axis=0, tiled=True)  87.5 us
    psum x1, waiting for transfers between devices, on_device(): normed_grad = lax.psum(input_part, 'col')  32.2 us
    dot_general x1, matrix products, on_device(): jnp.einsum('icj,jck->ick', panel_part, lax.all_gather(right_side, 'ia', a...  25.2 us
    dot_general x1, local copies, waits for them, and re-layouts, on_device(): jnp.einsum('icj,ick->jck', panel_part, left_side, preferred_element_type=...  16.6 us
    dot_general x1, matrix products, on_device(): jnp.einsum('icj,ick->jck', panel_part, left_side, preferred_element_type=...  14.1 us
  transfers between devices with their start and end apart: 5, of which 5 were waited for; matrix products, arithmetic and copies ran while one was open for 4% of the time, Pallas kernels for 0%

commit v1 on v0

--- a/solution.py
+++ b/solution.py
@@ -58,7 +58,7 @@
         - jnp.mean(scaled, axis=-1, keepdims=True)
         - unit_rows * jnp.mean(scaled * unit_rows, axis=-1, keepdims=True)
     )
-    summed = lax.psum(grad_part, ("ia", "ja"))
+    summed = jnp.sum(lax.all_gather(grad_part, ("ia", "ja")), axis=0)
     squares = lax.psum(jnp.sum(summed * summed), "col")
     factor = jnp.minimum(1.0, CLIP_LIMIT * lax.rsqrt(squares + 1e-06))
     weight_grads = summed * factor

time: 668 us -> 623 us (0.933)
  waiting for transfers between devices: 502 us -> 457 us
    psum x1 -> x0, waiting for transfers between devices: 99 us -> none  [on_device(): summed = lax.psum(grad_part, ('ia', 'ja'))]
    all_gather x0 -> x1, waiting for transfers between devices: none -> 54.1 us  [on_device(): summed = jnp.sum(lax.all_gather(grad_part, ('ia', 'ja')), axis=0)]
where the time goes in v1:
time: 623 us; the launch traced here: 615 us
  waiting for transfers between devices  457 us (73%)
  matrix products  55.9 us (9%)
  other arithmetic  49.3 us (8%)
  local copies, waits for them, and re-layouts  34.2 us (5%)
  between operations  14.9 us (2%)
    reduce_scatter x1, waiting for transfers between devices, on_device(): lax.psum_scatter(jnp.einsum('icj,ick->jck', panel_part, left_side, prefer...  154 us
    all_gather x1, waiting for transfers between devices, on_device(): row_panel = lax.all_gather(product_grad, 'ja', axis=2, tiled=True)  130 us
    all_gather x1, waiting for transfers between devices, on_device(): lax.all_gather(right_side, 'ia', axis=0, tiled=True)  87.5 us
    all_gather x1, waiting for transfers between devices, on_device(): summed = jnp.sum(lax.all_gather(grad_part, ('ia', 'ja')), axis=0)  54.1 us
    psum x1, waiting for transfers between devices, on_device(): normed_grad = lax.psum(input_part, 'col')  32 us
    dot_general x1, matrix products, on_device(): jnp.einsum('icj,jck->ick', panel_part, lax.all_gather(right_side, 'ia', a...  25.2 us
    dot_general x1, local copies, waits for them, and re-layouts, on_device(): jnp.einsum('icj,ick->jck', panel_part, left_side, preferred_element_type=...  16.6 us
    dot_general x1, matrix products, on_device(): jnp.einsum('icj,ick->jck', panel_part, left_side, preferred_element_type=...  14.1 us
  transfers between devices with their start and end apart: 5, of which 5 were waited for; matrix products, arithmetic and copies ran while one was open for 4% of the time, Pallas kernels for 0%

profile of v1, /device:TPU:0, one launch (start us, length us, event | category | flops | bytes accessed | tf_op | source)
XLA Modules:
  0.0 615.1 jit_solution(763372565973488246)
XLA Ops:
  7.2 4.3 copy.18
  11.8 3.5 convert_reduce_fusion
  15.3 4.8 fusion.10
  20.2 4.7 convolution_bitcast_fusion
  24.9 5.9 copy-done.1
  30.8 2.6 multiply_convert_fusion.5
  33.9 129.6 %all-gather.7.cloned.1.call-done = bf16[128,64,512]{2,0,1:T(8,128)(2,1)} async-done(((bf16[128,64,128]{2,0,1:T(8,128)(2,1)}), bf16[128,64,512]{2,0,1:T(8,128)(2,1)}) %all-gather.7.cloned.1.call-update) | async-done | bytes 8388624 | tf_op jit(solution)/shard_map/all_gather | solution.py:32
  163.5 87.5 %all-gather.5.cloned.1.call-done = bf16[512,64,128]{2,1,0:T(8,128)(2,1)} async-done(((bf16[128,64,128]{2,1,0:T(8,128)(2,1)}), bf16[512,64,128]{2,1,0:T(8,128)(2,1)}) %all-gather.5.cloned.1.call-update) | async-done | bytes 8388624 | tf_op jit(solution)/shard_map/all_gather | solution.py:37
  251.0 25.2 %fusion.11 = f32[64,128,128]{2,1,0:T(8,128)} fusion(bf16[128,64,512]{2,0,1:T(8,128)(2,1)} %all-gather.7.cloned.1.call-done, bf16[512,64,128]{2,1,0:T(8,128)(2,1)} %all-gather.5.cloned.1.call-done), kind=kOutput, calls=%fused_computation.15 | convolution fusion | flops 1073741824 | bytes 20971520 | tf_op jit(solution)/shard_map/icj,jck->ick/dot_general | solution.py:34
  276.2 5.4 copy.20
  281.6 6.8 %fusion.28 = (bf16[1,128,64,128]{3,2,1,0:T(8,128)(2,1)S(1)}, bf16[1,128,64,128]{3,2,1,0:T(8,128)(2,1)}, bf16[128,64,128]{2,1,0:T(8,128)(2,1)S(1)}) fusion(f32[64,128,128]{1,0,2:T(8,128)} %copy.20, f32[128,128]{1,0:T(8,128)S(1)} %broadcast_multiply_fusion.1, f32[4,128,64,128]{3,2,0,1:T(8,128)} %copy-done.1), kind=kLoop, calls=%fused_computation.43 | loop fusion | flops 14680064 | bytes 18939904 | tf_op jit(solution)/shard_map/stack | solution.py:49
  288.5 14.1 %fusion.32 = f32[64,128,512]{2,1,0:T(8,128)} fusion(bf16[128,64,512]{2,0,1:T(8,128)(2,1)} %all-gather.7.cloned.1.call-done, bf16[128,64,128]{2,1,0:T(8,128)(2,1)S(1)} %get-tuple-element.8), kind=kOutput, calls=%fused_computation.47 | convolution fusion | flops 1073741824 | bytes 27262976 | tf_op jit(solution)/shard_map/icj,ick->jck/dot_general | solution.py:42
  302.6 16.6 %copy.23 = f32[64,128,512]{1,0,2:T(8,128)} copy(f32[64,128,512]{2,1,0:T(8,128)} %fusion.32) | data formatting | bytes 33554432 | tf_op jit(solution)/shard_map/icj,ick->jck/dot_general | solution.py:42
  319.2 153.8 %reduce-scatter.2.cloned.1.call-done = f32[128,64,128]{2,1,0:T(8,128)} async-done(((f32[512,64,128]{2,1,0:T(8,128)}), f32[128,64,128]{2,1,0:T(8,128)}) %reduce-scatter.2.cloned.1.call-update) | async-done | bytes 4194320 | tf_op jit(solution)/shard_map/reduce_scatter | solution.py:41
  473.1 6.0 fusion.30
  479.2 1.3 copy-done.7
  481.1 5.4 fusion.34
  486.6 6.5 %convolution_bitcast_fusion.1 = f32[128,128,128]{2,1,0:T(8,128)} fusion(bf16[1,128,64,128]{3,2,1,0:T(8,128)(2,1)} %copy-done.8, bf16[1,128,64,128]{3,2,1,0:T(8,128)(2,1)} %copy-done.7, bf16[1,128,64,128]{3,2,1,0:T(8,128)(2,1)} %get-tuple-element.5, bf16[1,128,64,128]{3,2,1,0:T(8,128)(2,1)S(1)} %get-tuple-element.4, bf16[4,128,64]{1,2,0:T(8,128)(2,1)S(1)} %copy-done), kind=kOutput, calls=%fused_computation.42 | convolution fusion | flops 1086324736 | bytes 16842752 | tf_op jit(solution)/shard_map/wick,wdc->ikd/dot_general | solution.py:51
  493.1 54.1 %all-gather.9.cloned.1.call-done = f32[64,128,64]{1,2,0:T(8,128)} async-done(((f32[4,128,64]{1,2,0:T(8,128)}), f32[64,128,64]{1,2,0:T(8,128)}) %all-gather.9.cloned.1.call-update) | async-done | bytes 2097168 | tf_op jit(solution)/shard_map/all_gather | solution.py:61
  547.2 1.7 reduce_sum.58
  549.5 3.1 psum.15
  554.0 32.0 %all-reduce.2.cloned.1.call-done = f32[128,128,128]{2,1,0:T(8,128)} async-done(((f32[128,128,128]{2,1,0:T(8,128)}), f32[128,128,128]{2,1,0:T(8,128)}) %all-reduce.2.cloned.1.call-update) | async-done | bytes 8388624 | tf_op jit(solution)/shard_map/psum | solution.py:54
  586.0 11.6 %multiply_reduce_fusion = (f32[128,128]{1,0:T(8,128)S(1)}, f32[128,128]{1,0:T(8,128)S(1)}) fusion(f32[128,128,128]{2,1,0:T(8,128)} %all-reduce.2.cloned.1.call-done, f32[128]{0:T(128)S(1)} %copy-done.9, f32[128,128]{1,0:T(8,128)S(1)} %add_rsqrt_fusion, f32[128,128]{1,0:T(8,128)S(1)} %broadcast_multiply_fusion.4, bf16[128,128,128]{2,1,0:T(8,128)(2,1)} %param.5), kind=kLoop, calls=%fused_computation.17 | loop fusion | flops 14647296 | bytes 12845568 | tf_op jit(solution)/shard_map/reduce_sum | solution.py:58
  597.6 10.7 %fusion.9 = bf16[128,128,128]{2,1,0:T(8,128)(2,1)} fusion(bf16[128,128,128]{2,1,0:T(8,128)(2,1)S(1)} %copy-done.4, f32[128,128,128]{2,1,0:T(8,128)S(1)} %copy-done.5, f32[128,128]{1,0:T(8,128)S(1)} %get-tuple-element.11, f32[128,128]{1,0:T(8,128)S(1)} %get-tuple-element.12, f32[128]{0:T(128)S(1)} %copy-done.9, f32[128,128]{1,0:T(8,128)S(1)} %add_rsqrt_fusion, ...), kind=kLoop, calls=%fused_computation.12 | loop fusion | flops 18874368 | bytes 17039872 | tf_op jit(solution)/shard_map/convert_element_type | solution.py:65
  (38 shorter events, 3.0 us)
Async XLA Ops:
  7.2 13.0 %copy-start = (bf16[4,128,64]{1,2,0:T(8,128)(2,1)S(1)}, bf16[4,128,64]{1,2,0:T(8,128)(2,1)}, u32[]{:S(2)}) copy-start(bf16[4,128,64]{1,2,0:T(8,128)(2,1)} %param.7) | copy-start | bytes 196612
  7.2 4.4 copy-start.10
  7.2 156.3 %all-gather.7.cloned.1.call-start = ((), (), s32[]{:S(2)}) async-start(), calls=%async_computation.2 | async-start | bytes 10485760 | tf_op jit(solution)/shard_map/all_gather | solution.py:32
  11.5 239.5 %all-gather.5.cloned.1.call-start = ((), (), s32[]{:S(2)}) async-start(), calls=%async_computation.1 | async-start | bytes 10485760 | tf_op jit(solution)/shard_map/all_gather | solution.py:37
  11.6 3.7 copy-start.2
  11.8 8.4 %copy-start.9 = (f32[128]{0:T(128)S(1)}, f32[128]{0:T(128)}, u32[]{:S(2)}) copy-start(f32[128]{0:T(128)} %param.6) | copy-start | bytes 1540
  24.9 5.9 copy-start.1
  33.4 439.6 %reduce-scatter.2.cloned.1.call-start = ((), (), s32[]{:S(2)}) async-start(), calls=%async_computation.3 | async-start | bytes 20971520 | tf_op jit(solution)/shard_map/reduce_scatter | solution.py:41
  319.2 228.0 %all-gather.9.cloned.1.call-start = ((), (), s32[]{:S(2)}) async-start(), calls=%async_computation.5 | async-start | bytes 2228224 | tf_op jit(solution)/shard_map/all_gather | solution.py:61
  473.1 8.0 %copy-start.3 = (bf16[128,128,128]{2,1,0:T(8,128)(2,1)S(1)}, bf16[128,128,128]{2,1,0:T(8,128)(2,1)}, u32[]{:S(2)}) copy-start(bf16[128,128,128]{2,1,0:T(8,128)(2,1)} %param.5) | copy-start | bytes 12582916
  473.1 8.0 %copy-start.6 = (bf16[1,128,64,128]{3,2,1,0:T(8,128)(2,1)S(1)}, bf16[1,128,64,128]{3,2,1,0:T(8,128)(2,1)}, u32[]{:S(2)}) copy-start(bf16[1,128,64,128]{3,2,1,0:T(8,128)(2,1)} %get-tuple-element.5) | copy-start | bytes 6291460
  479.1 1.3 copy-start.7
  479.1 2.0 copy-start.8
  486.6 99.4 %all-reduce.2.cloned.1.call-start = ((), (), s32[]{:S(2)}) async-start(), calls=%async_computation.4 | async-start | bytes 16777216 | tf_op jit(solution)/shard_map/psum | solution.py:54
  586.0 11.6 %copy-start.4 = (bf16[128,128,128]{2,1,0:T(8,128)(2,1)S(1)}, bf16[128,128,128]{2,1,0:T(8,128)(2,1)}, u32[]{:S(2)}) copy-start(bf16[128,128,128]{2,1,0:T(8,128)(2,1)} %param.5) | copy-start | bytes 12582916
  586.0 11.6 %copy-start.5 = (f32[128,128,128]{2,1,0:T(8,128)S(1)}, f32[128,128,128]{2,1,0:T(8,128)}, u32[]{:S(2)}) copy-start(f32[128,128,128]{2,1,0:T(8,128)} %all-reduce.2.cloned.1.call-done) | copy-start | bytes 25165828
Sparse Core Ops, SparseCore 0:
  11.6 151.8 all-gather.6
  165.4 85.6 all-gather.4
  319.3 153.7 reduce-scatter.1
  486.7 60.4 all-gather.8
  549.5 36.4 all-reduce.1
